TPU v7x, 256 devices: a whole 4x4x8 slice. The times are simulated.
256 devices in a mesh: dp: 2 (over core), ret: 16 (over y, x), ctx: 8 (over z).
Axes of the slice: x: 4, y: 4, z: 8, core: 2. Of those that a mesh axis runs over, the one named last changes fastest.
Arguments:
- queries: bfloat16 [2, 8192, 4096], P('dp', 'ret', 'ctx'), may hold values from -6 to 6
- enc_states: bfloat16 [2, 32768, 896], P('dp', 'ret'), may hold values from -1600 to 1600
- w_key: bfloat16 [896, 4096], P(None, 'ctx'), may hold values from -0.1875 to 0.1875
- w_value: bfloat16 [896, 4096], P(None, 'ctx'), may hold values from -0.59765625 to 0.59765625
- shard_ids: int32 [2, 128, 2], P('dp', 'ret'), may hold values from 0 to 15, all different within a row; in each aligned block of 8 rows (0 to 7, 8 to 15, ..., all dimensions but the last counted through in order) at most 2 rows name the same one
- row_ids: int32 [2, 128, 2], P('dp', 'ret'), may hold values from 0 to 15
- grad_out: bfloat16 [2, 8192, 4096], P('dp', 'ret', 'ctx'), may hold values from -6 to 6
Outputs:
- attended: bfloat16 [2, 8192, 4096], P('dp', 'ret', 'ctx')
- grad_queries: bfloat16 [2, 8192, 4096], P('dp', 'ret', 'ctx')
- grad_w_key: float32 [896, 4096], P(('dp', 'ret'), 'ctx')
- grad_w_value: float32 [896, 4096], P(('dp', 'ret'), 'ctx')
Inputs may be any that keep to these rules, and one draw needn't show every extreme that they name: `shard_ids`: each block names 2 different shards; among the 8 blocks that one index of ret holds, no shard is named by more than 2 blocks, a bound that some block reaches.
All inputs are finite; a program needn't handle non-finite values.
Results may differ from a plain program's by a relative error of at most 0.019.
Values may be sent and summed in bfloat16 or wider, within the bound.
A program may use at most 128 MiB of HBM per device.

v0:
```python
import math
import jax
import jax.numpy as jnp
from jax import lax
from jax.sharding import PartitionSpec as P

HEAD_DIM = 128
NEIGH_LEN = 128
NEIGHBOURS = 2


def normalize_rows(states):
    floats = states.astype(jnp.float32)
    mean_square = jnp.mean(floats * floats, axis=-1, keepdims=True)
    return (floats * lax.rsqrt(mean_square + 1e-06)).astype(jnp.bfloat16)


def contract_rows(lhs_rows, rhs_rows):
    return lax.dot_general(
        lhs_rows, rhs_rows, (((0,), (0,)), ((), ())), preferred_element_type=jnp.float32
    )


def attend(query_block, key_block, value_block, grad_block):
    score_scale = 1.0 / math.sqrt(HEAD_DIM)
    scores = (
        jnp.einsum("cthd,cjhd->chtj", query_block, key_block, preferred_element_type=jnp.float32)
        * score_scale
    )
    exponent = jnp.exp(scores)
    denominator = jnp.sum(exponent, axis=-1)
    numerator = jnp.einsum(
        "chtj,cjhd->cthd",
        exponent.astype(jnp.bfloat16),
        value_block,
        preferred_element_type=jnp.float32,
    )
    output = numerator / jnp.transpose(denominator, (0, 2, 1))[..., None]
    prob_grad = jnp.einsum(
        "cthd,cjhd->chtj", grad_block, value_block, preferred_element_type=jnp.float32
    )
    row_delta = jnp.transpose(jnp.sum(grad_block.astype(jnp.float32) * output, axis=-1), (0, 2, 1))
    probability = exponent / denominator[..., None]
    score_grad = (probability * (prob_grad - row_delta[..., None]) * score_scale).astype(
        jnp.bfloat16
    )
    grad_query = jnp.einsum(
        "chtj,cjhd->cthd", score_grad, key_block, preferred_element_type=jnp.float32
    ).astype(jnp.bfloat16)
    grad_key = jnp.einsum(
        "chtj,cthd->cjhd", score_grad, query_block, preferred_element_type=jnp.float32
    ).astype(jnp.bfloat16)
    grad_value = jnp.einsum(
        "chtj,cthd->cjhd",
        probability.astype(jnp.bfloat16),
        grad_block,
        preferred_element_type=jnp.float32,
    ).astype(jnp.bfloat16)
    return (output.astype(jnp.bfloat16), grad_query, grad_key, grad_value)


def local(queries, enc_states, w_key, w_value, shard_ids, row_ids, grad_out):
    n_ret = lax.axis_size("ret")
    me_index = lax.axis_index("ret")
    blocks = shard_ids.shape[1]
    request_count = blocks * NEIGHBOURS
    capacity = request_count * 2 // n_ret
    feat_width = queries.shape[2]
    head_count = feat_width // HEAD_DIM
    db_dev = enc_states.shape[1] // NEIGH_LEN
    enc_width = enc_states.shape[2]
    context_rows = NEIGHBOURS * NEIGH_LEN
    every_shard, every_row = (
        lax.all_gather(shard_ids, "ret", axis=1, tiled=True),
        lax.all_gather(row_ids, "ret", axis=1, tiled=True),
    )
    req_shard = every_shard.reshape(n_ret, request_count)
    req_row = every_row.reshape(n_ret, request_count)
    positions = jnp.arange(request_count, dtype=jnp.int32)
    earlier = positions[None, :] < positions[:, None]
    same_shard = req_shard[:, :, None] == req_shard[:, None, :]
    slot_rank = jnp.sum((same_shard & earlier[None]).astype(jnp.int32), axis=2)
    own_shard = shard_ids.reshape(request_count)
    own_same = own_shard[:, None] == own_shard[None, :]
    own_rank = jnp.sum((own_same & earlier).astype(jnp.int32), axis=1)
    own_slot = own_shard * capacity + own_rank
    slot_iota = jnp.arange(capacity, dtype=jnp.int32)
    select = (req_shard[:, None, :] == me_index) & (
        slot_rank[:, None, :] == slot_iota[None, :, None]
    )
    filled = jnp.any(select, axis=2).reshape(-1)
    row_for = jnp.sum(jnp.where(select, req_row[:, None, :], 0), axis=2).reshape(-1)
    normed = normalize_rows(enc_states[0])
    normed_rows = normed.reshape(db_dev, NEIGH_LEN, enc_width)
    query_blocks = queries[0].reshape(blocks, -1, head_count, HEAD_DIM)
    grad_blocks = grad_out[0].reshape(blocks, -1, head_count, HEAD_DIM)
    both_weights = jnp.concatenate([w_key, w_value], axis=1)
    projected = jnp.dot(normed, both_weights, preferred_element_type=jnp.float32).astype(
        jnp.bfloat16
    )
    kv_table = projected.reshape(db_dev, NEIGH_LEN, 2 * feat_width)
    picked = jnp.take(kv_table, row_for, axis=0)
    outgoing = jnp.where(filled[:, None, None], picked, jnp.zeros_like(picked))
    outgoing = outgoing.reshape(n_ret, capacity, NEIGH_LEN, 2 * feat_width)
    incoming = lax.all_to_all(outgoing, "ret", split_axis=0, concat_axis=0, tiled=True)
    own_rows = jnp.take(
        incoming.reshape(n_ret * capacity, NEIGH_LEN, 2 * feat_width), own_slot, axis=0
    )
    own_rows = own_rows.reshape(blocks, context_rows, 2, head_count, HEAD_DIM)
    attended, grad_query, grad_key, grad_value = attend(
        query_blocks, own_rows[:, :, 0], own_rows[:, :, 1], grad_blocks
    )
    returned_grads = jnp.concatenate(
        [
            grad_key.reshape(request_count, NEIGH_LEN, feat_width),
            grad_value.reshape(request_count, NEIGH_LEN, feat_width),
        ],
        axis=2,
    )
    grad_slots = jnp.zeros((n_ret * capacity, NEIGH_LEN, 2 * feat_width), jnp.bfloat16)
    grad_slots = grad_slots.at[own_slot].set(returned_grads)
    arrived = lax.all_to_all(
        grad_slots.reshape(n_ret, capacity, NEIGH_LEN, 2 * feat_width),
        "ret",
        split_axis=0,
        concat_axis=0,
        tiled=True,
    )
    state_rows = jnp.take(normed_rows, row_for, axis=0)
    partial_value = contract_rows(
        state_rows.reshape(-1, enc_width), arrived.reshape(-1, 2 * feat_width)
    )
    summed = lax.psum_scatter(
        partial_value.astype(jnp.bfloat16), ("dp", "ret"), scatter_dimension=0, tiled=True
    ).astype(jnp.float32)
    grad_w_key = summed[:, :feat_width]
    grad_w_value = summed[:, feat_width:]
    return (
        attended.reshape(1, -1, feat_width),
        grad_query.reshape(1, -1, feat_width),
        grad_w_key,
        grad_w_value,
    )


def solution(mesh):
    placed = (
        P("dp", "ret", "ctx"),
        P("dp", "ret", None),
        P(None, "ctx"),
        P(None, "ctx"),
        P("dp", "ret", None),
        P("dp", "ret", None),
        P("dp", "ret", "ctx"),
    )
    return jax.shard_map(
        local,
        mesh=mesh,
        in_specs=placed,
        out_specs=(
            P("dp", "ret", "ctx"),
            P("dp", "ret", "ctx"),
            P(("dp", "ret"), "ctx"),
            P(("dp", "ret"), "ctx"),
        ),
        check_vma=False,
    )
```

profile of v0, /device:TPU:76, one launch (start us, length us, event | category | flops | bytes accessed | tf_op | source)
XLA Modules:
  0.0 476.9 jit_solution(10908282372569557570)
XLA Ops:
  1.6 22.1 %all_gather.6 = s32[1,128,2]{2,0,1:T(1,128)S(1)} all-gather(s32[1,8,2]{2,0,1:T(1,128)S(1)} %copy.67), channel_id=1, replica_groups=mesh['dp'=2,'ret'=16,'ctx'=8] {'ret'}, dimensions={1}, use_global_device_ids=true | all-gather | bytes 1088 | tf_op jit(solution)/shard_map/all_gather | solution.py:74
  26.2 21.5 %all_gather.7 = s32[1,128,2]{2,0,1:T(1,128)S(1)} all-gather(s32[1,8,2]{2,0,1:T(1,128)S(1)} %copy.69), channel_id=1, replica_groups=mesh['dp'=2,'ret'=16,'ctx'=8] {'ret'}, dimensions={1}, use_global_device_ids=true | all-gather | bytes 1088 | tf_op jit(solution)/shard_map/all_gather | solution.py:75
  52.1 8.4 %convolution_convert_fusion = bf16[2048,1024]{1,0:T(8,128)(2,1)} fusion(bf16[1,2048,896]{2,1,0:T(8,128)(2,1)} %param.8, f32[2048]{0:T(1024)S(1)} %get-tuple-element.9, bf16[896,512]{1,0:T(8,128)(2,1)S(1)} %copy-done.8, bf16[896,512]{1,0:T(8,128)(2,1)S(1)} %copy-done.9), kind=kOutput, calls=%fused_computation.13 | convolution fusion | flops 3769368576 | bytes 9707520 | tf_op jit(solution)/shard_map/dot_general | solution.py:98
  60.6 7.1 %gather_fusion = bf16[32,128,1024]{2,1,0:T(8,128)(2,1)} fusion(bf16[16,128,1024]{2,1,0:T(8,128)(2,1)} %bitcast.112, s32[1024]{0:T(1024)S(1)} %pad_clamp_fusion.1), kind=kCustom, calls=%fused_computation | custom fusion | bytes 16777344 | tf_op jit(solution)/shard_map/jit(_take)/gather | solution.py:102
  67.6 7.6 %select_select_fusion = bf16[16,2,128,1024]{3,2,1,0:T(8,128)(2,1)} fusion(bf16[16,2,128,1024]{3,2,1,0:T(8,128)(2,1)} %bitcast.111, pred[16,2]{1,0:T(8,128)(4,1)S(1)} %copy.70, pred[16,2]{1,0:T(8,128)(4,1)S(1)} %copy.68), kind=kLoop, calls=%fused_computation.4 | loop fusion | flops 8388608 | bytes 16777280 | tf_op jit(solution)/shard_map/jit(_where)/select_n | solution.py:103
  75.2 8.5 %all-to-all-start = ((bf16[16,2,128,1024]{3,2,1,0:T(8,128)(2,1)}), bf16[16,2,128,1024]{3,2,1,0:T(8,128)(2,1)}, u32[]{:S(2)}, u32[]{:S(2)}) async-start(bf16[16,2,128,1024]{3,2,1,0:T(8,128)(2,1)} %select_select_fusion), calls=%async_computation | async-start | bytes 16777216 | tf_op jit(solution)/shard_map/all_to_all | solution.py:105
  84.8 90.6 %all-to-all-done = bf16[16,2,128,1024]{3,2,1,0:T(8,128)(2,1)} async-done(((bf16[16,2,128,1024]{3,2,1,0:T(8,128)(2,1)}), bf16[16,2,128,1024]{3,2,1,0:T(8,128)(2,1)}, u32[]{:S(2)}, u32[]{:S(2)}) %all-to-all-start) | async-done | bytes 8388640 | tf_op jit(solution)/shard_map/all_to_all | solution.py:105
  175.3 6.2 %gather_fusion.1 = bf16[16,128,1024]{2,1,0:T(8,128)(2,1)} fusion(bf16[32,128,1024]{2,1,0:T(8,128)(2,1)} %bitcast.6, s32[1024]{0:T(1024)S(1)} %pad_clamp_fusion), kind=kCustom, calls=%fused_computation.1 | custom fusion | bytes 8388672 | tf_op jit(solution)/shard_map/jit(_take)/gather | solution.py:106
  181.5 7.7 %reshape.255 = bf16[8,256,2,4,128]{4,3,2,1,0:T(4,128)(2,1)} reshape(bf16[16,128,1024]{2,1,0:T(8,128)(2,1)} %gather_fusion.1) | data formatting | bytes 8388608 | tf_op jit(solution)/shard_map/jit(_take)/gather | solution.py:106
  201.8 4.1 reshape.217
  205.9 3.3 copy.84
  211.5 4.5 pad_maximum_fusion
  216.0 6.7 %copy.85 = bf16[16,128,1024]{2,1,0:T(8,128)(2,1)} copy(bf16[16,128,1024]{1,0,2:T(8,128)(2,1)} %pad_maximum_fusion) | data formatting | bytes 8388608 | tf_op jit(solution)/shard_map/concatenate | solution.py:113
  222.7 4.3 broadcast.174
  227.0 10.9 %scatter_fusion = bf16[32,128,1024]{2,1,0:T(8,128)(2,1)} fusion(bf16[32,128,1024]{2,1,0:T(8,128)(2,1)} %broadcast.174, s32[16]{0:T(128)S(1)} %fusion.27, bf16[16,128,1024]{2,1,0:T(8,128)(2,1)} %copy.85), kind=kCustom, calls=%fused_computation.3 | custom fusion | bytes 12582976 | tf_op jit(solution)/shard_map/scatter | solution.py:121
  237.8 9.6 %all-to-all-start.1 = ((bf16[16,2,128,1024]{3,2,1,0:T(8,128)(2,1)}), bf16[16,2,128,1024]{3,2,1,0:T(8,128)(2,1)}, u32[]{:S(2)}, u32[]{:S(2)}) async-start(bf16[16,2,128,1024]{3,2,1,0:T(8,128)(2,1)} %bitcast.110), calls=%async_computation.1 | async-start | bytes 16777216 | tf_op jit(solution)/shard_map/all_to_all | solution.py:122
  247.5 4.6 multiply_convert_fusion
  252.1 6.4 %gather_fusion.2 = bf16[32,128,896]{2,1,0:T(8,128)(2,1)} fusion(bf16[16,128,896]{2,1,0:T(8,128)(2,1)} %multiply_convert_fusion, s32[1024]{0:T(1024)S(1)} %pad_clamp_fusion.1), kind=kCustom, calls=%fused_computation.2 | custom fusion | bytes 14680192 | tf_op jit(solution)/shard_map/jit(_take)/gather | solution.py:129
  259.8 6.8 %broadcast_select_fusion = bf16[32,128,896]{2,1,0:T(8,128)(2,1)} fusion(bf16[32,128,896]{2,1,0:T(8,128)(2,1)} %gather_fusion.2, pred[32]{0:T(512)(128)(4,1)S(1)} %compare_and_fusion), kind=kLoop, calls=%fused_computation.10 | loop fusion | flops 3670016 | bytes 14680096 | tf_op jit(solution)/shard_map/jit(_take)/select_n | solution.py:129
  266.6 93.0 %all-to-all-done.1 = bf16[16,2,128,1024]{3,2,1,0:T(8,128)(2,1)} async-done(((bf16[16,2,128,1024]{3,2,1,0:T(8,128)(2,1)}), bf16[16,2,128,1024]{3,2,1,0:T(8,128)(2,1)}, u32[]{:S(2)}, u32[]{:S(2)}) %all-to-all-start.1) | async-done | bytes 8388640 | tf_op jit(solution)/shard_map/all_to_all | solution.py:122
  359.6 12.3 %convolution_convert_fusion.1 = bf16[896,1024]{1,0:T(8,128)(2,1)S(1)} fusion(bf16[4096,896]{1,0:T(8,128)(2,1)} %bitcast.114, bf16[4096,1024]{1,0:T(8,128)(2,1)} %bitcast.23), kind=kOutput, calls=%fused_computation.34 | convolution fusion | flops 7517110272 | bytes 17563648 | tf_op jit(solution)/shard_map/dot_general | solution.py:19
  371.9 80.4 %fusion = bf16[32,1024]{1,0:T(8,128)(2,1)S(1)} fusion(bf16[896,1024]{1,0:T(8,128)(2,1)S(1)} %convolution_convert_fusion.1), kind=kCustom, calls=%all-reduce-scatter | all-reduce-scatter fusion | flops 1048577 | bytes 1901568
  458.1 4.4 collective-permute-start.2
  462.6 8.0 %collective-permute-start.3 = (bf16[28,1024]{1,0:T(8,128)(2,1)S(1)}, bf16[28,1024]{1,0:T(8,128)(2,1)S(1)}, u32[]{:S(2)}, u32[]{:S(2)}) collective-permute-start(bf16[28,1024]{1,0:T(8,128)(2,1)S(1)} %slice.26), channel_id=1, source_target_pairs={{0,32},{8,40},{16,48},{24,56},{32,64},{40,72},{48,80},{56,88},{64,... | collective-permute-start | bytes 172040
  (81 shorter events, 36.4 us)
Async XLA Ops:
  0.6 51.5 %copy-start.8 = (bf16[896,512]{1,0:T(8,128)(2,1)S(1)}, bf16[896,512]{1,0:T(8,128)(2,1)}, u32[]{:S(2)}) copy-start(bf16[896,512]{1,0:T(8,128)(2,1)} %param.10) | copy-start | bytes 2752516
  0.6 51.5 %copy-start.9 = (bf16[896,512]{1,0:T(8,128)(2,1)S(1)}, bf16[896,512]{1,0:T(8,128)(2,1)}, u32[]{:S(2)}) copy-start(bf16[896,512]{1,0:T(8,128)(2,1)} %param.9) | copy-start | bytes 2752516
  75.2 8.5 %copy-start.6 = (s32[1,8,2]{1,2,0:T(2,128)S(1)}, s32[1,8,2]{1,2,0:T(2,128)}, u32[]{:S(2)}) copy-start(s32[1,8,2]{1,2,0:T(2,128)} %param.11) | copy-start | bytes 196
  75.2 9.2 %copy-start.3 = (bf16[1,512,512]{2,1,0:T(8,128)(2,1)S(1)}, bf16[1,512,512]{2,1,0:T(8,128)(2,1)}, u32[]{:S(2)}) copy-start(bf16[1,512,512]{2,1,0:T(8,128)(2,1)} %param.7) | copy-start | bytes 1572868
  75.2 9.3 %copy-start.4 = (bf16[1,512,512]{2,1,0:T(8,128)(2,1)S(1)}, bf16[1,512,512]{2,1,0:T(8,128)(2,1)}, u32[]{:S(2)}) copy-start(bf16[1,512,512]{2,1,0:T(8,128)(2,1)} %param.13) | copy-start | bytes 1572868
  75.2 100.1 %all-to-all-start = ((bf16[16,2,128,1024]{3,2,1,0:T(8,128)(2,1)}), bf16[16,2,128,1024]{3,2,1,0:T(8,128)(2,1)}, u32[]{:S(2)}, u32[]{:S(2)}) async-start(bf16[16,2,128,1024]{3,2,1,0:T(8,128)(2,1)} %select_select_fusion), calls=%async_computation | async-start | bytes 16777216 | tf_op jit(solution)/shard_map/all_to_all | solution.py:105
  84.5 107.6 %copy-start.1 = (bf16[8,64,4,128]{3,2,1,0:T(4,128)(2,1)}, bf16[8,64,4,128]{3,2,1,0:T(4,128)(2,1)S(1)}, u32[]{:S(2)}) copy-start(bf16[8,64,4,128]{3,2,1,0:T(4,128)(2,1)S(1)} %reshape_squeeze.6) | copy-start | bytes 1572868
  192.1 5.0 %copy-start = (bf16[8,256,2,4,128]{4,1,3,0,2:T(8,128)(2,1)}, bf16[8,256,2,4,128]{4,1,3,0,2:T(8,128)(2,1)S(1)}, u32[]{:S(2)}) copy-start(bf16[8,256,2,4,128]{4,1,3,0,2:T(8,128)(2,1)S(1)} %copy_select_fusion) | copy-start | bytes 12582916
  197.1 1.0 copy-start.2
  237.8 121.8 %all-to-all-start.1 = ((bf16[16,2,128,1024]{3,2,1,0:T(8,128)(2,1)}), bf16[16,2,128,1024]{3,2,1,0:T(8,128)(2,1)}, u32[]{:S(2)}, u32[]{:S(2)}) async-start(bf16[16,2,128,1024]{3,2,1,0:T(8,128)(2,1)} %bitcast.110), calls=%async_computation.1 | async-start | bytes 16777216 | tf_op jit(solution)/shard_map/all_to_all | solution.py:122
  252.1 6.4 %copy-start.7 = (u32[256]{0:T(256)S(1)}, u32[256]{0:T(256)}, u32[]{:S(2)}) copy-start(u32[256]{0:T(256)} %constant.73) | copy-start | bytes 3076
  452.3 21.7 %copy-start.5 = (bf16[8,64,4,128]{3,1,2,0:T(8,128)(2,1)S(1)}, bf16[8,64,4,128]{3,1,2,0:T(8,128)(2,1)}, u32[]{:S(2)}) copy-start(bf16[8,64,4,128]{3,1,2,0:T(8,128)(2,1)} %get-tuple-element.5) | copy-start | bytes 1572868
  452.4 23.1 %collective-permute-start = (bf16[32,1024]{1,0:T(8,128)(2,1)S(1)}, bf16[32,1024]{1,0:T(8,128)(2,1)S(1)}, u32[]{:S(2)}, u32[]{:S(2)}) collective-permute-start(bf16[32,1024]{1,0:T(8,128)(2,1)S(1)} %fusion), channel_id=1, source_target_pairs={{0,8},{8,16},{16,24},{24,32},{32,40},{40,48},{48,56},{56,64},{64,7... | collective-permute-start | bytes 196616
  454.8 20.7 %collective-permute-start.1 = (bf16[32,1024]{1,0:T(8,128)(2,1)S(1)}, bf16[32,1024]{1,0:T(8,128)(2,1)S(1)}, u32[]{:S(2)}, u32[]{:S(2)}) collective-permute-start(bf16[32,1024]{1,0:T(8,128)(2,1)S(1)} %fusion), channel_id=1, source_target_pairs={{0,16},{8,24},{16,32},{24,40},{32,48},{40,56},{48,64},{56,72},{64,... | collective-permute-start | bytes 196616
  458.1 17.4 %collective-permute-start.2 = (bf16[32,1024]{1,0:T(8,128)(2,1)S(1)}, bf16[32,1024]{1,0:T(8,128)(2,1)S(1)}, u32[]{:S(2)}, u32[]{:S(2)}) collective-permute-start(bf16[32,1024]{1,0:T(8,128)(2,1)S(1)} %fusion), channel_id=1, source_target_pairs={{0,24},{8,32},{16,40},{24,48},{32,56},{40,64},{48,72},{56,80},{64,... | collective-permute-start | bytes 196616
  462.6 12.9 %collective-permute-start.3 = (bf16[28,1024]{1,0:T(8,128)(2,1)S(1)}, bf16[28,1024]{1,0:T(8,128)(2,1)S(1)}, u32[]{:S(2)}, u32[]{:S(2)}) collective-permute-start(bf16[28,1024]{1,0:T(8,128)(2,1)S(1)} %slice.26), channel_id=1, source_target_pairs={{0,32},{8,40},{16,48},{24,56},{32,64},{40,72},{48,80},{56,88},{64,... | collective-permute-start | bytes 172040
where the time goes:
time: 478 us; the launch traced here: 477 us
  waiting for transfers between devices  184 us (38%)
  blocking collectives  124 us (26%)
  local copies, waits for them, and re-layouts  70.2 us (15%)
  starting transfers between devices  36.2 us (8%)
  other arithmetic  31.8 us (7%)
  matrix products  29.6 us (6%)
    all_to_all x1, waiting for transfers between devices, local(): lax.all_to_all(grad_slots.reshape(n_ret, capacity, NEIGH_LEN, 2 * feat_wi...  93 us
    all_to_all x1, waiting for transfers between devices, local(): lax.all_to_all(outgoing, 'ret', split_axis=0, concat_axis=0, tiled=True)  90.6 us
    unnamed x1, blocking collectives  80.4 us
    all_gather x1, blocking collectives, local(): lax.all_gather(shard_ids, 'ret', axis=1, tiled=True)  22.1 us
    all_gather x1, blocking collectives, local(): lax.all_gather(row_ids, 'ret', axis=1, tiled=True)  21.5 us
    unnamed x4, starting transfers between devices  18.2 us
    gather x2, local copies, waits for them, and re-layouts, local(): jnp.take(incoming.reshape(n_ret * capacity, NEIGH_LEN, 2 * feat_width), o...  13.9 us
    dot_general x1, matrix products, contract_rows(): lax.dot_general(lhs_rows, rhs_rows, (((0,), (0,)), ((), ())), preferred_e...  12.3 us
  transfers between devices with their start and end apart: 6, of which 2 were waited for; matrix products, arithmetic and copies ran while one was open for 5% of the time, Pallas kernels for 0%

commit v1 on v0

--- a/solution.py
+++ b/solution.py
@@ -7,6 +7,27 @@
 HEAD_DIM = 128
 NEIGH_LEN = 128
 NEIGHBOURS = 2
+
+
+def ring_gather(x, axis, dim):
+    size, position, extent = (lax.axis_size(axis), lax.axis_index(axis), x.shape[dim])
+    right = [(i, (i + 1) % size) for i in range(size)]
+    behind = [(i, (i - 1) % size) for i in range(size)]
+    out = jnp.zeros((*x.shape[:dim], size * extent, *x.shape[dim + 1 :]), x.dtype)
+    out = lax.dynamic_update_slice_in_dim(out, x, position * extent, axis=dim)
+    from_left = from_right = x
+    middle = size // 2
+    for hop in range(1, middle + 1):
+        from_left = lax.ppermute(from_left, axis, right)
+        out = lax.dynamic_update_slice_in_dim(
+            out, from_left, (position - hop) % size * extent, axis=dim
+        )
+        if hop < size - middle:
+            from_right = lax.ppermute(from_right, axis, behind)
+            out = lax.dynamic_update_slice_in_dim(
+                out, from_right, (position + hop) % size * extent, axis=dim
+            )
+    return out
 
 
 def normalize_rows(states):
@@ -72,7 +93,7 @@
     context_rows = NEIGHBOURS * NEIGH_LEN
     every_shard, every_row = (
         lax.all_gather(shard_ids, "ret", axis=1, tiled=True),
-        lax.all_gather(row_ids, "ret", axis=1, tiled=True),
+        ring_gather(row_ids, "ret", 1),
     )
     req_shard = every_shard.reshape(n_ret, request_count)
     req_row = every_row.reshape(n_ret, request_count)

time: 478 us -> 514 us (1.075)
  starting transfers between devices: 36.2 us -> 66.5 us
  blocking collectives: 124 us -> 102 us
  waiting for transfers between devices: 184 us -> 204 us
    all_gather x1 -> x0, blocking collectives: 21.5 us -> none  [local(): lax.all_gather(row_ids, 'ret', axis=1, tiled=True)]
    ppermute x0 -> x15, waiting for transfers between devices: none -> 19.9 us  [the longest x7 10.4 us: ring_gather(): from_right = lax.ppermute(from_right, axis, behind)]
    ppermute x0 -> x15, starting transfers between devices: none -> 19.5 us  [the longest x8 18.4 us: ring_gather(): from_left = lax.ppermute(from_left, axis, right)]
    all_to_all x1, starting transfers between devices: 8.48 us -> 19 us  [local(): lax.all_to_all(outgoing, 'ret', split_axis=0, concat_axis=0, tiled=True)]
  transfers between devices with their start and end apart: 6 -> 21, of which waited for: 2 -> 14; matrix products, arithmetic and copies ran while one was open for 5% -> 8% of each run, Pallas kernels for 0% -> 0%
where the time goes in v1:
time: 514 us; the launch traced here: 513 us
  waiting for transfers between devices  204 us (40%)
  blocking collectives  102 us (20%)
  local copies, waits for them, and re-layouts  75.3 us (15%)
  starting transfers between devices  66.5 us (13%)
  matrix products  32.9 us (6%)
  other arithmetic  30.4 us (6%)
    all_to_all x1, waiting for transfers between devices, local(): lax.all_to_all(grad_slots.reshape(n_ret, capacity, NEIGH_LEN, 2 * feat_wi...  96.2 us
    all_to_all x1, waiting for transfers between devices, local(): lax.all_to_all(outgoing, 'ret', split_axis=0, concat_axis=0, tiled=True)  87.9 us
    unnamed x1, blocking collectives  79 us
    all_gather x1, blocking collectives, local(): lax.all_gather(shard_ids, 'ret', axis=1, tiled=True)  22.9 us
    unnamed x4, starting transfers between devices  20 us
    all_to_all x1, starting transfers between devices, local(): lax.all_to_all(outgoing, 'ret', split_axis=0, concat_axis=0, tiled=True)  19 us
    ppermute x8, starting transfers between devices, ring_gather(): from_left = lax.ppermute(from_left, axis, right)  18.4 us
    gather x2, local copies, waits for them, and re-layouts, local(): jnp.take(incoming.reshape(n_ret * capacity, NEIGH_LEN, 2 * feat_width), o...  13.9 us
  transfers between devices with their start and end apart: 21, of which 14 were waited for; matrix products, arithmetic and copies ran while one was open for 8% of the time, Pallas kernels for 0%

profile of v1, /device:TPU:76, one launch (start us, length us, event | category | flops | bytes accessed | tf_op | source)
XLA Modules:
  0.0 512.5 jit_solution(11346525840622739190)
XLA Ops:
  4.3 22.9 %all_gather.3 = s32[1,128,2]{2,0,1:T(1,128)S(1)} all-gather(s32[1,8,2]{2,0,1:T(1,128)S(1)} %copy.112), channel_id=1, replica_groups=mesh['dp'=2,'ret'=16,'ctx'=8] {'ret'}, dimensions={1}, use_global_device_ids=true | all-gather | bytes 1088 | tf_op jit(solution)/shard_map/all_gather | solution.py:95
  32.1 8.4 %convolution_convert_fusion = bf16[2048,1024]{1,0:T(8,128)(2,1)} fusion(bf16[1,2048,896]{2,1,0:T(8,128)(2,1)} %param.8, f32[2048]{0:T(1024)S(1)} %get-tuple-element.9, bf16[896,512]{1,0:T(8,128)(2,1)S(1)} %copy-done.11, bf16[896,512]{1,0:T(8,128)(2,1)S(1)} %copy-done.12), kind=kOutput, calls=%fused_computation.13 | convolution fusion | flops 3769368576 | bytes 9707520 | tf_op jit(solution)/shard_map/dot_general | solution.py:119
  46.2 4.1 collective-permute-start.4
  79.6 7.1 %gather_fusion = bf16[32,128,1024]{2,1,0:T(8,128)(2,1)} fusion(bf16[16,128,1024]{2,1,0:T(8,128)(2,1)} %bitcast.111, s32[1024]{0:T(1024)S(1)} %pad_clamp_fusion.1), kind=kCustom, calls=%fused_computation | custom fusion | bytes 16777344 | tf_op jit(solution)/shard_map/jit(_take)/gather | solution.py:123
  86.7 7.6 %select_select_fusion = bf16[16,2,128,1024]{3,2,1,0:T(8,128)(2,1)} fusion(bf16[16,2,128,1024]{3,2,1,0:T(8,128)(2,1)} %bitcast.110, pred[16,2]{1,0:T(8,128)(4,1)S(1)} %copy.130, pred[16,2]{1,0:T(8,128)(4,1)S(1)} %copy.113), kind=kLoop, calls=%fused_computation.4 | loop fusion | flops 8388608 | bytes 16777280 | tf_op jit(solution)/shard_map/jit(_where)/select_n | solution.py:124
  94.3 19.0 %all-to-all-start = ((bf16[16,2,128,1024]{3,2,1,0:T(8,128)(2,1)}), bf16[16,2,128,1024]{3,2,1,0:T(8,128)(2,1)}, u32[]{:S(2)}, u32[]{:S(2)}) async-start(bf16[16,2,128,1024]{3,2,1,0:T(8,128)(2,1)} %select_select_fusion), calls=%async_computation | async-start | bytes 16777216 | tf_op jit(solution)/shard_map/all_to_all | solution.py:126
  114.4 87.9 %all-to-all-done = bf16[16,2,128,1024]{3,2,1,0:T(8,128)(2,1)} async-done(((bf16[16,2,128,1024]{3,2,1,0:T(8,128)(2,1)}), bf16[16,2,128,1024]{3,2,1,0:T(8,128)(2,1)}, u32[]{:S(2)}, u32[]{:S(2)}) %all-to-all-start) | async-done | bytes 8388640 | tf_op jit(solution)/shard_map/all_to_all | solution.py:126
  202.3 6.2 %gather_fusion.1 = bf16[16,128,1024]{2,1,0:T(8,128)(2,1)} fusion(bf16[32,128,1024]{2,1,0:T(8,128)(2,1)} %bitcast.6, s32[1024]{0:T(1024)S(1)} %pad_clamp_fusion), kind=kCustom, calls=%fused_computation.1 | custom fusion | bytes 8388672 | tf_op jit(solution)/shard_map/jit(_take)/gather | solution.py:127
  208.4 7.7 %reshape.255 = bf16[8,256,2,4,128]{4,3,2,1,0:T(4,128)(2,1)} reshape(bf16[16,128,1024]{2,1,0:T(8,128)(2,1)} %gather_fusion.1) | data formatting | bytes 8388608 | tf_op jit(solution)/shard_map/jit(_take)/gather | solution.py:127
  241.3 4.2 reshape.217
  245.5 3.9 pad_maximum_fusion
  249.4 6.8 %copy.145 = bf16[16,128,1024]{2,1,0:T(8,128)(2,1)} copy(bf16[16,128,1024]{1,0,2:T(8,128)(2,1)} %pad_maximum_fusion) | data formatting | bytes 8388608 | tf_op jit(solution)/shard_map/concatenate | solution.py:134
  256.2 4.3 broadcast.189
  260.5 10.9 %scatter_fusion = bf16[32,128,1024]{2,1,0:T(8,128)(2,1)} fusion(bf16[32,128,1024]{2,1,0:T(8,128)(2,1)} %broadcast.189, s32[16]{0:T(128)S(1)} %fusion.27, bf16[16,128,1024]{2,1,0:T(8,128)(2,1)} %copy.145), kind=kCustom, calls=%fused_computation.3 | custom fusion | bytes 12582976 | tf_op jit(solution)/shard_map/scatter | solution.py:142
  271.4 8.1 %all-to-all-start.1 = ((bf16[16,2,128,1024]{3,2,1,0:T(8,128)(2,1)}), bf16[16,2,128,1024]{3,2,1,0:T(8,128)(2,1)}, u32[]{:S(2)}, u32[]{:S(2)}) async-start(bf16[16,2,128,1024]{3,2,1,0:T(8,128)(2,1)} %bitcast.109), calls=%async_computation.1 | async-start | bytes 16777216 | tf_op jit(solution)/shard_map/all_to_all | solution.py:143
  280.7 4.6 multiply_convert_fusion
  285.4 6.4 %gather_fusion.2 = bf16[32,128,896]{2,1,0:T(8,128)(2,1)} fusion(bf16[16,128,896]{2,1,0:T(8,128)(2,1)} %multiply_convert_fusion, s32[1024]{0:T(1024)S(1)} %pad_clamp_fusion.1), kind=kCustom, calls=%fused_computation.2 | custom fusion | bytes 14680192 | tf_op jit(solution)/shard_map/jit(_take)/gather | solution.py:150
  291.8 6.8 %broadcast_select_fusion = bf16[32,128,896]{2,1,0:T(8,128)(2,1)} fusion(bf16[32,128,896]{2,1,0:T(8,128)(2,1)} %gather_fusion.2, pred[32]{0:T(512)(128)(4,1)S(1)} %compare_and_fusion), kind=kLoop, calls=%fused_computation.10 | loop fusion | flops 3670016 | bytes 14680096 | tf_op jit(solution)/shard_map/jit(_take)/select_n | solution.py:150
  298.6 96.2 %all-to-all-done.1 = bf16[16,2,128,1024]{3,2,1,0:T(8,128)(2,1)} async-done(((bf16[16,2,128,1024]{3,2,1,0:T(8,128)(2,1)}), bf16[16,2,128,1024]{3,2,1,0:T(8,128)(2,1)}, u32[]{:S(2)}, u32[]{:S(2)}) %all-to-all-start.1) | async-done | bytes 8388640 | tf_op jit(solution)/shard_map/all_to_all | solution.py:143
  394.8 12.3 %convolution_convert_fusion.1 = bf16[896,1024]{1,0:T(8,128)(2,1)S(1)} fusion(bf16[4096,896]{1,0:T(8,128)(2,1)} %bitcast.113, bf16[4096,1024]{1,0:T(8,128)(2,1)} %bitcast.23), kind=kOutput, calls=%fused_computation.34 | convolution fusion | flops 7517110272 | bytes 17563648 | tf_op jit(solution)/shard_map/dot_general | solution.py:40
  407.2 79.0 %fusion = bf16[32,1024]{1,0:T(8,128)(2,1)S(1)} fusion(bf16[896,1024]{1,0:T(8,128)(2,1)S(1)} %convolution_convert_fusion.1), kind=kCustom, calls=%all-reduce-scatter | all-reduce-scatter fusion | flops 1048577 | bytes 1901568
  486.2 4.4 collective-permute-start.15
  492.5 5.5 %collective-permute-start.17 = (bf16[32,1024]{1,0:T(8,128)(2,1)S(1)}, bf16[32,1024]{1,0:T(8,128)(2,1)S(1)}, u32[]{:S(2)}, u32[]{:S(2)}) collective-permute-start(bf16[32,1024]{1,0:T(8,128)(2,1)S(1)} %fusion), channel_id=1, source_target_pairs={{0,24},{8,32},{16,40},{24,48},{32,56},{40,64},{48,72},{56,80},{64,... | collective-permute-start | bytes 196616
  498.0 8.2 %collective-permute-start.18 = (bf16[28,1024]{1,0:T(8,128)(2,1)S(1)}, bf16[28,1024]{1,0:T(8,128)(2,1)S(1)}, u32[]{:S(2)}, u32[]{:S(2)}) collective-permute-start(bf16[28,1024]{1,0:T(8,128)(2,1)S(1)} %slice.26), channel_id=1, source_target_pairs={{0,32},{8,40},{16,48},{24,56},{32,64},{40,72},{48,80},{56,88},{64,... | collective-permute-start | bytes 172040
  (151 shorter events, 78.6 us)
Async XLA Ops:
  0.6 31.5 %copy-start.11 = (bf16[896,512]{1,0:T(8,128)(2,1)S(1)}, bf16[896,512]{1,0:T(8,128)(2,1)}, u32[]{:S(2)}) copy-start(bf16[896,512]{1,0:T(8,128)(2,1)} %param.10) | copy-start | bytes 2752516
  0.7 39.9 %collective-permute-start = (s32[1,8,2]{1,2,0:T(2,128)}, s32[1,8,2]{1,2,0:T(2,128)S(1)}, u32[]{:S(2)}, u32[]{:S(2)}) collective-permute-start(s32[1,8,2]{1,2,0:T(2,128)} %param.12), channel_id=1, source_target_pairs={{0,8},{8,16},{16,24},{24,32},{32,40},{40,48},{48,56},{56,64},{64,7... | collective-permute-start | bytes 200 | tf_op jit(solution)/shard_map/ppermute | solution.py:21
  1.9 38.7 %collective-permute-start.1 = (s32[1,8,2]{1,2,0:T(2,128)}, s32[1,8,2]{1,2,0:T(2,128)S(1)}, u32[]{:S(2)}, u32[]{:S(2)}) collective-permute-start(s32[1,8,2]{1,2,0:T(2,128)} %param.12), channel_id=1, source_target_pairs={{0,120},{8,0},{16,8},{24,16},{32,24},{40,32},{48,40},{56,48},{64,5... | collective-permute-start | bytes 200 | tf_op jit(solution)/shard_map/ppermute | solution.py:26
  40.7 3.6 collective-permute-start.2
  42.5 3.6 collective-permute-start.3
  46.2 5.4 %collective-permute-start.4 = (s32[1,8,2]{1,2,0:T(2,128)S(1)}, s32[1,8,2]{1,2,0:T(2,128)S(1)}, u32[]{:S(2)}, u32[]{:S(2)}) collective-permute-start(s32[1,8,2]{1,2,0:T(2,128)S(1)} %collective-permute-done.2), channel_id=1, source_target_pairs={{0,8},{8,16},{16,24},{24,32},{32,40},{40,48},{48,56},{56,64},{64,7... | collective-permute-start | bytes 200 | tf_op jit(solution)/shard_map/ppermute | solution.py:21
  50.4 3.6 collective-permute-start.5
  54.0 3.6 collective-permute-start.6
  56.2 3.6 collective-permute-start.7
  59.9 3.6 collective-permute-start.8
  62.1 3.6 collective-permute-start.9
  65.8 3.7 collective-permute-start.10
  68.1 3.6 collective-permute-start.11
  71.8 3.6 collective-permute-start.12
  74.0 3.7 collective-permute-start.13
  75.5 3.6 collective-permute-start.14
  94.3 108.0 %all-to-all-start = ((bf16[16,2,128,1024]{3,2,1,0:T(8,128)(2,1)}), bf16[16,2,128,1024]{3,2,1,0:T(8,128)(2,1)}, u32[]{:S(2)}, u32[]{:S(2)}) async-start(bf16[16,2,128,1024]{3,2,1,0:T(8,128)(2,1)} %select_select_fusion), calls=%async_computation | async-start | bytes 16777216 | tf_op jit(solution)/shard_map/all_to_all | solution.py:126
  114.1 104.9 %copy-start.3 = (bf16[8,64,4,128]{3,2,1,0:T(4,128)(2,1)}, bf16[8,64,4,128]{3,2,1,0:T(4,128)(2,1)S(1)}, u32[]{:S(2)}) copy-start(bf16[8,64,4,128]{3,2,1,0:T(4,128)(2,1)S(1)} %reshape_squeeze.6) | copy-start | bytes 1572868
  114.2 117.2 %copy-start.8 = (bf16[8,64,4,128]{3,2,1,0:T(4,128)(2,1)}, bf16[8,64,4,128]{3,2,1,0:T(4,128)(2,1)S(1)}, u32[]{:S(2)}) copy-start(bf16[8,64,4,128]{3,2,1,0:T(4,128)(2,1)S(1)} %reshape_squeeze.7) | copy-start | bytes 1572868
  271.4 123.4 %all-to-all-start.1 = ((bf16[16,2,128,1024]{3,2,1,0:T(8,128)(2,1)}), bf16[16,2,128,1024]{3,2,1,0:T(8,128)(2,1)}, u32[]{:S(2)}, u32[]{:S(2)}) async-start(bf16[16,2,128,1024]{3,2,1,0:T(8,128)(2,1)} %bitcast.109), calls=%async_computation.1 | async-start | bytes 16777216 | tf_op jit(solution)/shard_map/all_to_all | solution.py:143
  486.2 24.9 %collective-permute-start.15 = (bf16[32,1024]{1,0:T(8,128)(2,1)S(1)}, bf16[32,1024]{1,0:T(8,128)(2,1)S(1)}, u32[]{:S(2)}, u32[]{:S(2)}) collective-permute-start(bf16[32,1024]{1,0:T(8,128)(2,1)S(1)} %fusion), channel_id=1, source_target_pairs={{0,8},{8,16},{16,24},{24,32},{32,40},{40,48},{48,56},{56,64},{64,7... | collective-permute-start | bytes 196616
  490.6 20.5 %collective-permute-start.16 = (bf16[32,1024]{1,0:T(8,128)(2,1)S(1)}, bf16[32,1024]{1,0:T(8,128)(2,1)S(1)}, u32[]{:S(2)}, u32[]{:S(2)}) collective-permute-start(bf16[32,1024]{1,0:T(8,128)(2,1)S(1)} %fusion), channel_id=1, source_target_pairs={{0,16},{8,24},{16,32},{24,40},{32,48},{40,56},{48,64},{56,72},{64,... | collective-permute-start | bytes 196616
  492.5 18.6 %collective-permute-start.17 = (bf16[32,1024]{1,0:T(8,128)(2,1)S(1)}, bf16[32,1024]{1,0:T(8,128)(2,1)S(1)}, u32[]{:S(2)}, u32[]{:S(2)}) collective-permute-start(bf16[32,1024]{1,0:T(8,128)(2,1)S(1)} %fusion), channel_id=1, source_target_pairs={{0,24},{8,32},{16,40},{24,48},{32,56},{40,64},{48,72},{56,80},{64,... | collective-permute-start | bytes 196616
  498.0 13.1 %collective-permute-start.18 = (bf16[28,1024]{1,0:T(8,128)(2,1)S(1)}, bf16[28,1024]{1,0:T(8,128)(2,1)S(1)}, u32[]{:S(2)}, u32[]{:S(2)}) collective-permute-start(bf16[28,1024]{1,0:T(8,128)(2,1)S(1)} %slice.26), channel_id=1, source_target_pairs={{0,32},{8,40},{16,48},{24,56},{32,64},{40,72},{48,80},{56,88},{64,... | collective-permute-start | bytes 172040
  (12 other events, 139.2 us)
